TPU v7x, 32 devices: a whole 2x2x4 slice. The times are simulated.
32 devices in a mesh: seq: 8 (over z, x), fsdp: 4 (over y, core).
Axes of the slice: x: 2, y: 2, z: 4, core: 2. Of those that a mesh axis runs over, the one named last changes fastest.
Arguments:
- tokens: bfloat16 [4, 1024, 1536], P('fsdp', 'seq'), may hold values from -6 to 6
- in_weight: bfloat16 [1536, 6400], P('fsdp'), may hold values from -0.15625 to 0.15625
- step_weight: bfloat16 [1536, 48], P('fsdp'), may hold values from -0.15625 to 0.15625
- conv_kernel: bfloat16 [4, 3328], P(None, 'fsdp'), may hold values from -3 to 3
- conv_bias: bfloat16 [3328], P('fsdp'), may hold values from -3 to 3
- step_bias: bfloat16 [48], P('fsdp'), may hold values from -6 to -3
- log_decay: bfloat16 [48], P('fsdp'), may hold values from -7 to 1
- skip_gain: bfloat16 [48], P('fsdp'), may hold values from 0.5 to 1.5
- gate_gain: bfloat16 [3072], P('fsdp'), may hold values from 0.5 to 1.5
- norm_gain: bfloat16 [1536], P('fsdp'), may hold values from 0.5 to 1.5
- out_weight: bfloat16 [3072, 1536], P('fsdp'), may hold values from -0.109375 to 0.109375
- cotangent: bfloat16 [4, 1024, 1536], P('fsdp', 'seq'), may hold values from -6 to 6
Outputs:
- block_out: bfloat16 [4, 1024, 1536], P('fsdp', 'seq')
- input_grad: float32 [4, 1024, 1536], P('fsdp', 'seq')
- in_weight_grad: float32 [1536, 6400], P('fsdp')
- step_weight_grad: float32 [1536, 48], P('fsdp')
- conv_kernel_grad: float32 [4, 3328], P(None, 'fsdp')
- conv_bias_grad: float32 [3328], P('fsdp')
- step_bias_grad: float32 [48], P('fsdp')
- log_decay_grad: float32 [48], P('fsdp')
- skip_gain_grad: float32 [48], P('fsdp')
- gate_gain_grad: float32 [3072], P('fsdp')
- norm_gain_grad: float32 [1536], P('fsdp')
- out_weight_grad: float32 [3072, 1536], P('fsdp')
All inputs are finite; a program needn't handle non-finite values.
Results may differ from a plain program's by a relative error of at most 0.012.
The roundings to bfloat16 on the way count: a program that leaves them out, or rounds other values in their place, can miss the bound.
Values may be sent and summed in bfloat16 or wider, within the bound.
A program may use at most 320 MiB of HBM per device.

v0:
```python
import jax
import jax.numpy as jnp
from jax import lax
from jax.sharding import PartitionSpec as P

N = 128
BLOCK = 256
epsilon = 1e-05
highest = lax.Precision.HIGHEST


def block_step(carried, pieces, decay_rate):
    x_blk, step_blk, b_blk, c_blk = pieces
    cumulative = jnp.cumsum(step_blk * decay_rate[None, :], axis=0).T
    positions = jnp.arange(step_blk.shape[0])
    triangle = positions[:, None] >= positions[None, :]
    log_gap = jnp.where(triangle[None], cumulative[:, :, None] - cumulative[:, None, :], -1e30)
    scores = jnp.dot(c_blk, b_blk.T, precision=highest)
    mixing = jnp.exp(log_gap) * scores[None] * step_blk.T[:, None, :]
    y_inside = jnp.einsum("hij,jhp->ihp", mixing, x_blk, precision=highest)
    y_carried = jnp.exp(cumulative).T[:, :, None] * jnp.einsum(
        "in,hpn->ihp", c_blk, carried, precision=highest
    )
    weighting = jnp.exp(cumulative[:, -1:] - cumulative) * step_blk.T
    renewed = jnp.exp(cumulative[:, -1])[:, None, None] * carried + jnp.einsum(
        "hj,jhp,jn->hpn", weighting, x_blk, b_blk, precision=highest
    )
    return (renewed, y_inside + y_carried)


def ssd_scan(x_heads, step_size, decay_rate, b_conv, c_conv, carried):
    length = step_size.shape[0]
    extent = min(BLOCK, length)
    number = length // extent
    pieces = (
        x_heads.reshape((number, extent) + x_heads.shape[1:]),
        step_size.reshape((number, extent) + step_size.shape[1:]),
        b_conv.reshape(number, extent, -1),
        c_conv.reshape(number, extent, -1),
    )

    def advance(ssm_state, block_in):
        return block_step(ssm_state, block_in, decay_rate)

    finals, outputs = lax.scan(jax.checkpoint(advance), carried, pieces)
    return outputs.reshape(x_heads.shape)


def prepare(extended, raw_steps, conv_kernel, conv_offset, step_bias, log_rates):
    kernel_width = conv_kernel.shape[0]
    length = extended.shape[0] - kernel_width + 1
    summed = conv_offset[None, :] + sum(
        (
            conv_kernel[offset][None, :] * extended[offset : offset + length]
            for offset in range(kernel_width)
        )
    )
    active = jax.nn.silu(summed)
    split_at = active.shape[1] - 2 * N
    step_size = jax.nn.softplus(raw_steps + step_bias[None, :])
    return (
        active[:, :split_at],
        active[:, split_at : split_at + N],
        active[:, split_at + N :],
        step_size,
        -jnp.exp(log_rates),
    )


def mix_out(x_conv, b_conv, c_conv, step_size, decay_rate, gate_in, skip_part, carried):
    length, head_count = step_size.shape
    x_heads = x_conv.reshape(length, head_count, -1)
    result = (
        ssd_scan(x_heads, step_size, decay_rate, b_conv, c_conv, carried)
        + skip_part[None, :, None] * x_heads
    )
    return result.reshape(length, -1) * jax.nn.silu(gate_in)


def rms_forward(values, gains):
    scaling = lax.rsqrt(jnp.mean(values * values, axis=-1, keepdims=True) + epsilon)
    return (values * scaling * gains[None, :], scaling)


def rms_backward(values, gains, scaling, upstream):
    weighted = upstream * gains[None, :]
    gain_grad = jnp.sum(upstream * values * scaling, axis=0)
    inner_mean = jnp.mean(weighted * values, axis=-1, keepdims=True)
    return (scaling * weighted - scaling**3 * values * inner_mean, gain_grad)


def contract(left, right, left_dim, right_dim):
    return lax.dot_general(
        left, right, (((left_dim,), (right_dim,)), ((), ())), preferred_element_type=jnp.float32
    )


def reorder(gradient, axis_pos, outer_count, inner_count):
    moved_axis = jnp.moveaxis(gradient, axis_pos, 0)
    regrouped = moved_axis.reshape((outer_count, inner_count, -1) + moved_axis.shape[1:])
    swapped = jnp.swapaxes(regrouped, 0, 1).reshape(moved_axis.shape)
    return jnp.moveaxis(swapped, 0, axis_pos)


def place_slice(part, total_len, start_at, axis_pos):
    zeros_shape = part.shape[:axis_pos] + (total_len,) + part.shape[axis_pos + 1 :]
    anchor = tuple((start_at if index_pos == axis_pos else 0 for index_pos in range(part.ndim)))
    return lax.dynamic_update_slice(jnp.zeros(zeros_shape, jnp.float32), part, anchor)


def shards(
    tokens,
    in_weight,
    step_weight,
    conv_kernel,
    conv_bias,
    step_bias,
    log_decay,
    skip_gain,
    gate_gain,
    norm_gain,
    out_weight,
    cotangent,
):
    gathered = (
        lax.all_gather(in_weight, "fsdp", axis=0, tiled=True),
        lax.all_gather(step_weight, "fsdp", axis=0, tiled=True),
        lax.all_gather(conv_kernel, "fsdp", axis=1, tiled=True),
        lax.all_gather(conv_bias, "fsdp", axis=0, tiled=True),
        lax.all_gather(step_bias, "fsdp", axis=0, tiled=True),
        lax.all_gather(log_decay, "fsdp", axis=0, tiled=True),
        lax.all_gather(skip_gain, "fsdp", axis=0, tiled=True),
        lax.all_gather(gate_gain, "fsdp", axis=0, tiled=True),
        lax.all_gather(norm_gain, "fsdp", axis=0, tiled=True),
        lax.all_gather(out_weight, "fsdp", axis=0, tiled=True),
    )
    w_in = gathered[0]
    w_step = gathered[1]
    w_out = gathered[9]
    kernel_f = gathered[2].astype(jnp.float32)
    bias_f = gathered[3].astype(jnp.float32)
    step_bias_f = gathered[4].astype(jnp.float32)
    decay_f = gathered[5].astype(jnp.float32)
    skip_f = gathered[6].astype(jnp.float32)
    gate_f = gathered[7].astype(jnp.float32)
    norm_f = gathered[8].astype(jnp.float32)
    inner_width = w_out.shape[0]
    head_count = w_step.shape[1]
    head_size = inner_width // head_count
    kernel_width = kernel_f.shape[0]
    out_cotangent = cotangent[0]
    residual = tokens[0].astype(jnp.float32)
    normed, scale_in = rms_forward(residual, norm_f)
    hidden = normed.astype(jnp.bfloat16)
    projected = jnp.dot(hidden, w_in, preferred_element_type=jnp.float32).astype(jnp.bfloat16)
    raw_steps = jnp.dot(hidden, w_step, preferred_element_type=jnp.float32).astype(jnp.bfloat16)
    seq_count = lax.axis_size("seq")
    position = lax.axis_index("seq")
    head_group = head_count // seq_count
    columns = head_group * head_size
    col_start = position * columns
    head_start = position * head_group
    tiled_bc = jnp.tile(projected[:, 2 * inner_width :], (1, seq_count))
    gate_part, x_part, step_part, bc_part = (
        lax.all_to_all(projected[:, :inner_width], "seq", split_axis=1, concat_axis=0, tiled=True),
        lax.all_to_all(
            projected[:, inner_width : 2 * inner_width],
            "seq",
            split_axis=1,
            concat_axis=0,
            tiled=True,
        ),
        lax.all_to_all(raw_steps, "seq", split_axis=1, concat_axis=0, tiled=True),
        lax.all_to_all(tiled_bc, "seq", split_axis=1, concat_axis=0, tiled=True),
    )
    my_kernel = jnp.concatenate(
        [lax.dynamic_slice_in_dim(kernel_f, col_start, columns, 1), kernel_f[:, inner_width:]],
        axis=1,
    )
    my_bias = jnp.concatenate(
        [lax.dynamic_slice_in_dim(bias_f, col_start, columns, 0), bias_f[inner_width:]], axis=0
    )
    my_step_bias = lax.dynamic_slice_in_dim(step_bias_f, head_start, head_group, 0)
    my_decay = lax.dynamic_slice_in_dim(decay_f, head_start, head_group, 0)
    my_skip = lax.dynamic_slice_in_dim(skip_f, head_start, head_group, 0)
    padding = jnp.zeros((kernel_width - 1, columns + 2 * N), jnp.float32)
    extended = jnp.concatenate(
        [padding, jnp.concatenate([x_part, bc_part], axis=1).astype(jnp.float32)], axis=0
    )
    prepared, pull_prepare = jax.vjp(
        prepare, extended, step_part.astype(jnp.float32), my_kernel, my_bias, my_step_bias, my_decay
    )
    x_conv, b_conv, c_conv, step_size, decay_rate = prepared
    start_state = jnp.zeros((head_group, head_size, N), jnp.float32)
    gated_f, pull_mix = jax.vjp(
        mix_out,
        x_conv,
        b_conv,
        c_conv,
        step_size,
        decay_rate,
        gate_part.astype(jnp.float32),
        my_skip,
        start_state,
    )
    gated_out = lax.all_to_all(
        gated_f.astype(jnp.bfloat16), "seq", split_axis=0, concat_axis=1, tiled=True
    )
    gated_back = gated_out.astype(jnp.float32)
    mixed_f, scale_out = rms_forward(gated_back, gate_f)
    mixed_norm = mixed_f.astype(jnp.bfloat16)
    block_out = (residual + jnp.dot(mixed_norm, w_out, preferred_element_type=jnp.float32)).astype(
        jnp.bfloat16
    )
    out_grad = contract(mixed_norm, out_cotangent, 0, 0)
    mixed_grad = contract(out_cotangent, w_out, 1, 1)
    gated_grad, gate_gain_grad = rms_backward(gated_back, gate_f, scale_out, mixed_grad)
    gated_grad_b = lax.optimization_barrier(gated_grad.astype(jnp.bfloat16))
    gated_grad_h = lax.all_to_all(
        gated_grad_b, "seq", split_axis=1, concat_axis=0, tiled=True
    ).astype(jnp.float32)
    x_grad, b_grad, c_grad, step_grad, rate_grad, gate_in_grad, skip_grad_h, unused = pull_mix(
        gated_grad_h
    )
    ext_grad, raw_grad, kernel_grad_h, bias_grad_h, step_bias_grad_h, decay_grad_h = pull_prepare(
        (x_grad, b_grad, c_grad, step_grad, rate_grad)
    )
    body_grad = ext_grad[kernel_width - 1 :]
    gate_back, x_back, step_back = (
        lax.all_to_all(
            gate_in_grad.astype(jnp.bfloat16), "seq", split_axis=0, concat_axis=1, tiled=True
        ),
        lax.all_to_all(
            body_grad[:, :columns].astype(jnp.bfloat16),
            "seq",
            split_axis=0,
            concat_axis=1,
            tiled=True,
        ),
        lax.all_to_all(
            raw_grad.astype(jnp.bfloat16), "seq", split_axis=0, concat_axis=1, tiled=True
        ),
    )
    bc_back = lax.psum_scatter(
        body_grad[:, columns:].astype(jnp.bfloat16), "seq", scatter_dimension=0, tiled=True
    )
    proj_grad = jnp.concatenate([gate_back, x_back, bc_back], axis=1)
    kernel_grad = jnp.concatenate(
        [
            place_slice(kernel_grad_h[:, :columns], inner_width, col_start, 1),
            kernel_grad_h[:, columns:],
        ],
        axis=1,
    )
    bias_grad = jnp.concatenate(
        [place_slice(bias_grad_h[:columns], inner_width, col_start, 0), bias_grad_h[columns:]],
        axis=0,
    )
    step_bias_grad = place_slice(step_bias_grad_h, head_count, head_start, 0)
    decay_grad = place_slice(decay_grad_h, head_count, head_start, 0)
    skip_grad = place_slice(skip_grad_h, head_count, head_start, 0)
    in_grad = contract(hidden, proj_grad, 0, 0)
    step_w_grad = contract(hidden, step_back, 0, 0)
    hidden_grad = contract(proj_grad, w_in, 1, 1) + contract(step_back, w_step, 1, 1)
    resid_grad, norm_gain_grad = rms_backward(residual, norm_f, scale_in, hidden_grad)
    input_grad = out_cotangent.astype(jnp.float32) + resid_grad
    fsdp_count = lax.axis_size("fsdp")
    seq_total = lax.axis_size("seq")

    def spread_heads(gradient):
        return jnp.tile(gradient.reshape(fsdp_count, -1), (seq_total, 1)).reshape(-1)

    blocks = (
        lax.psum_scatter(
            reorder(in_grad, 0, fsdp_count, seq_total),
            ("seq", "fsdp"),
            scatter_dimension=0,
            tiled=True,
        ),
        lax.psum_scatter(
            reorder(step_w_grad, 0, fsdp_count, seq_total),
            ("seq", "fsdp"),
            scatter_dimension=0,
            tiled=True,
        ),
        lax.psum_scatter(
            reorder(kernel_grad, 1, fsdp_count, seq_total),
            ("seq", "fsdp"),
            scatter_dimension=1,
            tiled=True,
        ),
        lax.psum_scatter(
            reorder(bias_grad, 0, fsdp_count, seq_total),
            ("seq", "fsdp"),
            scatter_dimension=0,
            tiled=True,
        ),
        lax.psum_scatter(
            spread_heads(step_bias_grad), ("seq", "fsdp"), scatter_dimension=0, tiled=True
        ),
        lax.psum_scatter(
            spread_heads(decay_grad), ("seq", "fsdp"), scatter_dimension=0, tiled=True
        ),
        lax.psum_scatter(spread_heads(skip_grad), ("seq", "fsdp"), scatter_dimension=0, tiled=True),
        lax.psum_scatter(
            reorder(gate_gain_grad, 0, fsdp_count, seq_total),
            ("seq", "fsdp"),
            scatter_dimension=0,
            tiled=True,
        ),
        lax.psum_scatter(
            reorder(norm_gain_grad, 0, fsdp_count, seq_total),
            ("seq", "fsdp"),
            scatter_dimension=0,
            tiled=True,
        ),
        lax.psum_scatter(
            reorder(out_grad, 0, fsdp_count, seq_total),
            ("seq", "fsdp"),
            scatter_dimension=0,
            tiled=True,
        ),
    )
    joined = (
        lax.all_gather(blocks[0], "seq", axis=0, tiled=True),
        lax.all_gather(blocks[1], "seq", axis=0, tiled=True),
        lax.all_gather(blocks[2], "seq", axis=1, tiled=True),
        lax.all_gather(blocks[3], "seq", axis=0, tiled=True),
        lax.all_gather(blocks[7], "seq", axis=0, tiled=True),
        lax.all_gather(blocks[8], "seq", axis=0, tiled=True),
        lax.all_gather(blocks[9], "seq", axis=0, tiled=True),
    )
    totals = (
        joined[0],
        joined[1],
        joined[2],
        joined[3],
        blocks[4],
        blocks[5],
        blocks[6],
        joined[4],
        joined[5],
        joined[6],
    )
    return (
        block_out[None],
        input_grad[None],
        totals[0],
        totals[1],
        totals[2],
        totals[3],
        totals[4],
        totals[5],
        totals[6],
        totals[7],
        totals[8],
        totals[9],
    )


def solution(mesh):
    placed = (
        P("fsdp", "seq", None),
        P("fsdp", None),
        P("fsdp", None),
        P(None, "fsdp"),
        P("fsdp"),
        P("fsdp"),
        P("fsdp"),
        P("fsdp"),
        P("fsdp"),
        P("fsdp"),
        P("fsdp", None),
        P("fsdp", "seq", None),
    )
    return jax.shard_map(
        shards,
        mesh=mesh,
        in_specs=placed,
        out_specs=(
            P("fsdp", "seq", None),
            P("fsdp", "seq", None),
            P("fsdp", None),
            P("fsdp", None),
            P(None, "fsdp"),
            P("fsdp"),
            P("fsdp"),
            P("fsdp"),
            P("fsdp"),
            P("fsdp"),
            P("fsdp"),
            P("fsdp", None),
        ),
        check_vma=False,
    )
```

profile of v0, /device:TPU:0, one launch (start us, length us, event | category | flops | bytes accessed | tf_op | source)
XLA Modules:
  0.0 1683.6 jit_solution(14580512450812876870)
XLA Ops:
  28.3 108.3 %all-gather.9.cloned.1.call-done = bf16[1536,6400]{1,0:T(8,128)(2,1)} async-done(((bf16[384,6400]{1,0:T(8,128)(2,1)}), bf16[1536,6400]{1,0:T(8,128)(2,1)}) %all-gather.9.cloned.1.call-update) | async-done | bytes 19660816 | tf_op jit(solution)/shard_map/all_gather | solution.py:126
  154.5 12.8 all-to-all-done.2
  211.3 74.2 %while.41 = (s32[]{:T(128)}, f32[6,64,128]{2,1,0:T(8,128)S(1)}, f32[4,256,6,64]{1,0,3,2:T(4,128)}, f32[4,6,64,128]{3,2,1,0:T(8,128)}, f32[4,256,6]{1,2,0:T(8,128...) while((s32[]{:T(128)}, f32[6,64,128]{2,1,0:T(8,128)S(1)}, ...), condition=%wide.region_4.5_spmd.clone, body=%wide.region_1.4_spmd.clone.sunk | while | flops 706957824 | bytes 5773208 | solution.py:45
  310.4 14.1 all-to-all-done.4
  346.8 14.6 all-to-all-done.5
  376.5 167.4 %while.42 = (s32[]{:T(128)}, f32[6]{0:T(128)}, f32[6,64,128]{2,1,0:T(8,128)S(1)}, f32[4,256,6,64]{1,0,3,2:T(4,128)}, f32[4,256,6]{1,2,0:T(8,128)}, /*index=5*/f3...) while((s32[]{:T(128)}, f32[6]{0:T(128)}, ...), condition=%wide.region_20.21_spmd.clone, body=%wide.region_7.20_spmd.clone.sunk | while | flops 1669247488 | bytes 18030544 | solution.py:45
  402.7 9.5 dynamic_update_slice.93
  444.6 9.5 dynamic_update_slice.93
  528.3 9.5 dynamic_update_slice.93
  575.7 9.9 all_to_all.141
  595.2 13.1 all-to-all-done.6
  613.6 21.0 %all-to-all-done.7 = bf16[8,128,384]{2,1,0:T(8,128)(2,1)} async-done(((bf16[8,128,384]{2,1,0:T(8,128)(2,1)}), bf16[8,128,384]{2,1,0:T(8,128)(2,1)}, u32[]{:S(2)}, u32[]{:S(2)}) %all-to-all-start.7) | async-done | bytes 786464 | tf_op jit(solution)/shard_map/all_to_all | solution.py:233
  639.3 12.3 fusion.152
  653.8 20.1 %convolution_bitcast_fusion.2 = f32[8,4,48,6400]{3,2,0,1:T(8,128)} fusion(bf16[4,8,48,128]{3,2,1,0:T(8,128)(2,1)S(1)} %bitcast.577, bf16[128,6400]{1,0:T(8,128)(2,1)} %constant_dynamic-update-slice_fusion), kind=kOutput, calls=%fused_computation.128 | convolution fusion | flops 2516582400 | bytes 41353216 | tf_op jit(solution)/shard_map/dot_general | solution.py:93
  673.9 28.6 %copy.323 = f32[8,4,48,6400]{3,2,1,0:T(8,128)} copy(f32[8,4,48,6400]{3,2,0,1:T(8,128)} %convolution_bitcast_fusion.2) | data formatting | bytes 78643200 | tf_op jit(solution)/shard_map/transpose | solution.py:101
  711.7 130.3 %reduce-scatter.12.cloned.1.call-done = f32[96,1536]{1,0:T(8,128)} async-done(((f32[3072,1536]{1,0:T(8,128)}), f32[96,1536]{1,0:T(8,128)}) %reduce-scatter.12.cloned.1.call-update) | async-done | bytes 589840 | tf_op jit(solution)/shard_map/reduce_scatter | solution.py:317
  842.1 364.2 %reduce-scatter.10.cloned.1.call-done = f32[48,6400]{1,0:T(8,128)} async-done(((f32[1536,6400]{1,0:T(8,128)}), f32[48,6400]{1,0:T(8,128)}) %reduce-scatter.10.cloned.1.call-update) | async-done | bytes 1228816 | tf_op jit(solution)/shard_map/reduce_scatter | solution.py:274
  1214.8 123.9 %all-reduce.33.cloned.1.call-done = (f32[4,3328]{1,0:T(4,128)}, f32[3328]{0:T(1024)}, f32[384]{0:T(512)}, f32[384]{0:T(512)}, f32[384]{0:T(512)}, /*index=5*/f32[3072]{0:T(1024)}, f32[1536]{0:T(1024)}) async-done(((f32[4,3328]{1,0:T(4,128)}, f32[3328]{0:T(1024)}, f32[384]{0:T(512)}, f32[384]{0:T(512)}, f32[384]{0:T(512)}, /*index=5*/f32[3072]{0:T(1024)}, f32[1536]{0:T(1024)}), (f32[4,3328]{1,0:T(4,128)}, ...) | async-done | bytes 89616
  1339.5 27.0 %all-gather.3 = f32[8,104,4]{1,2,0:T(4,128)S(1)} all-gather(f32[1,104,4]{1,2,0:T(4,128)S(1)} %dynamic-slice_bitcast_fusion.7), channel_id=1, replica_groups=mesh['seq'=8,'fsdp'=4] {'seq'}, dimensions={0}, use_global_device_ids=true | all-gather | bytes 14976 | tf_op jit(solution)/shard_map/all_gather | solution.py:327
  1373.5 35.5 %all-reduce.29 = (f32[832]{0:T(1024)}, f32[768]{0:T(1024)}, f32[384]{0:T(512)}) all-reduce(f32[832]{0:T(1024)S(1)} %dynamic-slice_dynamic-update-slice_fusion.2, f32[768]{0:T(1024)S(1)} %dynamic-slice_dynamic-update-slice_fusion.1, f32[384]{0:T(512)S(1)} %dynamic-slice_dynamic-update-slice_fusion), channel_id=1, replica_groups=mesh['seq'=8,'fsdp'=4] {'seq'}, use_global_device_ids=true, to_apply=%add.18 | all-reduce | flops 1984 | bytes 15872
  1409.1 32.7 %reduce-scatter.14.cloned.1.call-done = f32[48,48]{1,0:T(8,128)} async-done(((f32[1536,48]{1,0:T(8,128)}), f32[48,48]{1,0:T(8,128)}) %reduce-scatter.14.cloned.1.call-update) | async-done | bytes 9232 | tf_op jit(solution)/shard_map/reduce_scatter | solution.py:280
  1441.8 32.1 %all_gather.62 = f32[384,48]{1,0:T(8,128)S(1)} all-gather(f32[48,48]{1,0:T(8,128)} %reduce-scatter.14.cloned.1.call-done), channel_id=1, replica_groups=mesh['seq'=8,'fsdp'=4] {'seq'}, dimensions={0}, use_global_device_ids=true | all-gather | bytes 82944 | tf_op jit(solution)/shard_map/all_gather | solution.py:326
  1474.6 48.8 %all-gather.15.cloned.1.call-done = f32[768,1536]{1,0:T(8,128)} async-done(((f32[96,1536]{1,0:T(8,128)}), f32[768,1536]{1,0:T(8,128)}) %all-gather.15.cloned.1.call-update) | async-done | bytes 4718608 | tf_op jit(solution)/shard_map/all_gather | solution.py:331
  1523.4 142.8 %all-gather.13.cloned.1.call-done = f32[384,6400]{1,0:T(8,128)} async-done(((f32[48,6400]{1,0:T(8,128)}), f32[384,6400]{1,0:T(8,128)}) %all-gather.13.cloned.1.call-update) | async-done | bytes 9830416 | tf_op jit(solution)/shard_map/all_gather | solution.py:325
  (656 shorter events, 442.9 us)
Async XLA Ops:
  7.2 129.5 %all-gather.9.cloned.1.call-start = ((), (), s32[]{:S(2)}) async-start(), calls=%async_computation.13 | async-start | bytes 24576000 | tf_op jit(solution)/shard_map/all_gather | solution.py:126
  14.2 122.5 %copy-start.41 = (f32[1536]{0:T(1024)}, f32[1536]{0:T(1024)S(1)}, u32[]{:S(2)}) copy-start(f32[1536]{0:T(1024)S(1)} %reshape.548) | copy-start | bytes 18436
  20.7 116.0 %copy-start.58 = (f32[128]{0:T(128)}, f32[128]{0:T(128)S(1)}, u32[]{:S(2)}) copy-start(f32[128]{0:T(128)S(1)} %get-tuple-element.798) | copy-start | bytes 1540
  21.6 124.5 %all-to-all-start = ((bf16[128,8,6]{0,2,1:T(8,128)(2,1)}), bf16[128,8,6]{0,2,1:T(8,128)(2,1)S(1)}, u32[]{:S(2)}, u32[]{:S(2)}) async-start(bf16[128,8,6]{0,2,1:T(8,128)(2,1)} %all_to_all.106), calls=%async_computation | async-start | bytes 32768 | tf_op jit(solution)/shard_map/all_to_all | solution.py:173
  27.6 297.5 %all-gather.11.cloned.1.call-start = ((), (), s32[]{:S(2)}) async-start(), calls=%async_computation.14 | async-start | bytes 11796480 | tf_op jit(solution)/shard_map/all_gather | solution.py:135
  146.9 20.4 %all-to-all-start.2 = ((bf16[128,8,256]{2,0,1:T(8,128)(2,1)}), bf16[128,8,256]{2,0,1:T(8,128)(2,1)S(1)}, u32[]{:S(2)}, u32[]{:S(2)}) async-start(bf16[128,8,256]{2,0,1:T(8,128)(2,1)} %tile.28), calls=%async_computation.2 | async-start | bytes 1048576 | tf_op jit(solution)/shard_map/all_to_all | solution.py:174
  167.4 24.0 %all-to-all-start.1 = ((bf16[128,8,384]{2,0,1:T(8,128)(2,1)}), bf16[128,8,384]{2,0,1:T(8,128)(2,1)S(1)}, u32[]{:S(2)}, u32[]{:S(2)}) async-start(bf16[128,8,384]{2,0,1:T(8,128)(2,1)} %bitcast.418), calls=%async_computation.1 | async-start | bytes 1572864 | tf_op jit(solution)/shard_map/all_to_all | solution.py:166
  181.1 160.6 %copy-start.68 = (f32[48]{0:T(128)}, f32[48]{0:T(128)S(1)}, u32[]{:S(2)}) copy-start(f32[48]{0:T(128)S(1)} %convert_element_type.138) | copy-start | bytes 580
  187.1 108.4 %copy-start.55 = (f32[384]{0:T(512)}, f32[384]{0:T(512)S(1)}, u32[]{:S(2)}) copy-start(f32[384]{0:T(512)S(1)} %mul.640) | copy-start | bytes 4612
  191.4 99.3 %all-to-all-start.3 = ((bf16[128,8,384]{0,2,1:T(8,128)(2,1)}), bf16[128,8,384]{0,2,1:T(8,128)(2,1)}, u32[]{:S(2)}, u32[]{:S(2)}) async-start(bf16[128,8,384]{0,2,1:T(8,128)(2,1)} %bitcast.18), calls=%async_computation.3 | async-start | bytes 1572864 | tf_op jit(solution)/shard_map/all_to_all | solution.py:165
  298.9 25.6 %all-to-all-start.4 = ((bf16[8,128,384]{2,1,0:T(8,128)(2,1)}), bf16[8,128,384]{2,1,0:T(8,128)(2,1)S(1)}, u32[]{:S(2)}, u32[]{:S(2)}) async-start(bf16[8,128,384]{2,1,0:T(8,128)(2,1)} %bitcast.580), calls=%async_computation.4 | async-start | bytes 1572864 | tf_op jit(solution)/shard_map/all_to_all | solution.py:206
  337.4 24.1 %all-to-all-start.5 = ((bf16[128,8,384]{0,2,1:T(8,128)(2,1)}), bf16[128,8,384]{0,2,1:T(8,128)(2,1)}, u32[]{:S(2)}, u32[]{:S(2)}) async-start(bf16[128,8,384]{0,2,1:T(8,128)(2,1)} %bitcast.583), calls=%async_computation.5 | async-start | bytes 1572864 | tf_op jit(solution)/shard_map/all_to_all | solution.py:219
  341.6 296.2 %reduce-scatter.8.cloned.1.call-start = ((), (), s32[]{:S(2)}) async-start(), calls=%async_computation.15 | async-start | bytes 589824 | tf_op jit(solution)/shard_map/reduce_scatter | solution.py:244
  563.5 278.5 %reduce-scatter.12.cloned.1.call-start = ((), (), s32[]{:S(2)}) async-start(), calls=%async_computation.18 | async-start | bytes 19464192 | tf_op jit(solution)/shard_map/reduce_scatter | solution.py:317
  585.6 22.7 %all-to-all-start.6 = ((bf16[8,128,384]{2,1,0:T(8,128)(2,1)}), bf16[8,128,384]{2,1,0:T(8,128)(2,1)S(1)}, u32[]{:S(2)}, u32[]{:S(2)}) async-start(bf16[8,128,384]{2,1,0:T(8,128)(2,1)} %bitcast.29), calls=%async_computation.6 | async-start | bytes 1572864 | tf_op jit(solution)/shard_map/all_to_all | solution.py:230
  608.3 26.4 %all-to-all-start.7 = ((bf16[8,128,384]{2,1,0:T(8,128)(2,1)}), bf16[8,128,384]{2,1,0:T(8,128)(2,1)}, u32[]{:S(2)}, u32[]{:S(2)}) async-start(bf16[8,128,384]{2,1,0:T(8,128)(2,1)} %bitcast.584), calls=%async_computation.7 | async-start | bytes 1572864 | tf_op jit(solution)/shard_map/all_to_all | solution.py:233
  612.5 593.8 %reduce-scatter.10.cloned.1.call-start = ((), (), s32[]{:S(2)}) async-start(), calls=%async_computation.16 | async-start | bytes 40550400 | tf_op jit(solution)/shard_map/reduce_scatter | solution.py:274
  702.5 636.2 %all-reduce.33.cloned.1.call-start = ((), (), s32[]{:S(2)}) async-start(), calls=%async_computation.21 | async-start | bytes 192512
  710.4 731.4 %reduce-scatter.14.cloned.1.call-start = ((), (), s32[]{:S(2)}) async-start(), calls=%async_computation.20 | async-start | bytes 811008 | tf_op jit(solution)/shard_map/reduce_scatter | solution.py:280
  711.6 494.7 %copy-start.74 = (u32[32]{0:T(128)S(1)}, u32[32]{0:T(128)}, u32[]{:S(2)}) copy-start(u32[32]{0:T(128)} %constant.200) | copy-start | bytes 388
  711.6 497.3 %copy-start.36 = (f32[4,1,768]{2,1,0:T(1,128)S(1)}, f32[4,1,768]{2,1,0:T(1,128)}, u32[]{:S(2)}) copy-start(f32[4,1,768]{2,1,0:T(1,128)} %copy-done.35) | copy-start | bytes 36868
  711.6 497.3 %copy-start.61 = (f32[128]{0:T(128)S(1)}, f32[128]{0:T(128)}, u32[]{:S(2)}) copy-start(f32[128]{0:T(128)} %copy-done.60) | copy-start | bytes 1540
  711.7 811.7 %all-gather.15.cloned.1.call-start = ((), (), s32[]{:S(2)}) async-start(), calls=%async_computation.19 | async-start | bytes 5308416 | tf_op jit(solution)/shard_map/all_gather | solution.py:331
  842.1 824.1 %all-gather.13.cloned.1.call-start = ((), (), s32[]{:S(2)}) async-start(), calls=%async_computation.17 | async-start | bytes 11059200 | tf_op jit(solution)/shard_map/all_gather | solution.py:325
  (87 other events, 676.3 us)
Sparse Core Ops, SparseCore 0:
  9.6 127.0 all-gather.8
  138.2 64.7 all-gather.10
  563.6 63.3 reduce-scatter.7
  633.3 208.7 reduce-scatter.11
  848.3 357.9 reduce-scatter.9
  1213.8 124.8 all-reduce.32
  1344.4 97.3 reduce-scatter.13
  1444.0 79.3 all-gather.14
  1525.6 140.5 all-gather.12
where the time goes:
time: 1690 us; the launch traced here: 1680 us
  waiting for transfers between devices  1030 us (61%)
  local copies, waits for them, and re-layouts  232 us (14%)
  blocking collectives  135 us (8%)
  matrix products  132 us (8%)
  other arithmetic  96 us (6%)
  starting transfers between devices  38.3 us (2%)
  between operations  18.4 us (1%)
    reduce_scatter x1, waiting for transfers between devices, shards(): lax.psum_scatter(reorder(in_grad, 0, fsdp_count, seq_total), ('seq', 'fsd...  364 us
    all_gather x1, waiting for transfers between devices, shards(): lax.all_gather(blocks[0], 'seq', axis=0, tiled=True)  143 us
    reduce_scatter x1, waiting for transfers between devices, shards(): lax.psum_scatter(reorder(out_grad, 0, fsdp_count, seq_total), ('seq', 'fs...  130 us
    unnamed x10, waiting for transfers between devices  125 us
    all_gather x1, waiting for transfers between devices, shards(): lax.all_gather(in_weight, 'fsdp', axis=0, tiled=True)  108 us
    dynamic_update_slice x16, local copies, waits for them, and re-layouts, ssd_scan(): finals, outputs = lax.scan(jax.checkpoint(advance), carried, pieces)  79.5 us
    another operation x33, other arithmetic  50.7 us
    all_gather x1, waiting for transfers between devices, shards(): lax.all_gather(blocks[9], 'seq', axis=0, tiled=True)  48.8 us
  transfers between devices with their start and end apart: 17, of which 13 were waited for; matrix products, arithmetic and copies ran while one was open for 14% of the time, Pallas kernels for 0%

commit v1 on v0

--- a/solution.py
+++ b/solution.py
@@ -2,6 +2,7 @@
 import jax.numpy as jnp
 from jax import lax
 from jax.sharding import PartitionSpec as P
+from jax.lax import axis_index, ppermute, psum
 
 N = 128
 BLOCK = 256
@@ -122,8 +123,25 @@
     out_weight,
     cotangent,
 ):
+
+    def _update_series(field):
+        dev_axis = "fsdp"
+        amount_of = psum(1, dev_axis)
+        steps_seen = [field]
+        for i0 in range(1, amount_of):
+            steps_seen.append(
+                ppermute(
+                    steps_seen[i0 - 1],
+                    axis_name=dev_axis,
+                    perm=[(d, (d - 1) % amount_of) for d in range(amount_of)],
+                )
+            )
+        piece_now = jnp.concatenate(steps_seen, axis=0)
+        y_new = jnp.roll(piece_now, axis_index(dev_axis) * field.shape[0], axis=0)
+        return y_new
+
     gathered = (
-        lax.all_gather(in_weight, "fsdp", axis=0, tiled=True),
+        _update_series(in_weight),
         lax.all_gather(step_weight, "fsdp", axis=0, tiled=True),
         lax.all_gather(conv_kernel, "fsdp", axis=1, tiled=True),
         lax.all_gather(conv_bias, "fsdp", axis=0, tiled=True),

time: 1690 us -> 1800 us (1.065)
  blocking collectives: 135 us -> 198 us
  local copies, waits for them, and re-layouts: 232 us -> 272 us
  waiting for transfers between devices: 1030 us -> 1010 us
    all_gather x1 -> x0, waiting for transfers between devices: 108 us -> none  [shards(): lax.all_gather(in_weight, 'fsdp', axis=0, tiled=True)]
    ppermute x0 -> x3, waiting for transfers between devices: none -> 108 us  [_update_series(): ppermute(steps_seen[i0 - 1], axis_name=dev_axis, perm=[(d, (d - 1) % amou...]
    all_gather x1, blocking collectives: 6.18 us -> 55.3 us  [shards(): lax.all_gather(norm_gain, 'fsdp', axis=0, tiled=True)]
    unnamed x173 -> x198, local copies, waits for them, and re-layouts: 41.2 us -> 74.2 us
    all_to_all x1, waiting for transfers between devices: 21 us -> 1.41 us  [shards(): lax.all_to_all(raw_grad.astype(jnp.bfloat16), 'seq', split_axis=0, concat...]
    unnamed x10 -> x9, waiting for transfers between devices: 125 us -> 125 us
  transfers between devices with their start and end apart: 17 -> 19, of which waited for: 13 -> 14; matrix products, arithmetic and copies ran while one was open for 14% -> 15% of each run, Pallas kernels for 0% -> 0%
where the time goes in v1:
time: 1800 us; the launch traced here: 1780 us
  waiting for transfers between devices  1010 us (56%)
  local copies, waits for them, and re-layouts  272 us (15%)
  blocking collectives  198 us (11%)
  matrix products  132 us (7%)
  other arithmetic  105 us (6%)
  starting transfers between devices  43.4 us (2%)
  between operations  19 us (1%)
    reduce_scatter x1, waiting for transfers between devices, shards(): lax.psum_scatter(reorder(in_grad, 0, fsdp_count, seq_total), ('seq', 'fsd...  364 us
    all_gather x1, waiting for transfers between devices, shards(): lax.all_gather(blocks[0], 'seq', axis=0, tiled=True)  143 us
    reduce_scatter x1, waiting for transfers between devices, shards(): lax.psum_scatter(reorder(out_grad, 0, fsdp_count, seq_total), ('seq', 'fs...  129 us
    unnamed x9, waiting for transfers between devices  125 us
    ppermute x3, waiting for transfers between devices, _update_series(): ppermute(steps_seen[i0 - 1], axis_name=dev_axis, perm=[(d, (d - 1) % amou...  108 us
    dynamic_update_slice x16, local copies, waits for them, and re-layouts, ssd_scan(): finals, outputs = lax.scan(jax.checkpoint(advance), carried, pieces)  79.4 us
    unnamed x198, local copies, waits for them, and re-layouts  74.2 us
    all_gather x1, blocking collectives, shards(): lax.all_gather(norm_gain, 'fsdp', axis=0, tiled=True)  55.3 us
  transfers between devices with their start and end apart: 19, of which 14 were waited for; matrix products, arithmetic and copies ran while one was open for 15% of the time, Pallas kernels for 0%

profile of v1, /device:TPU:0, one launch (start us, length us, event | category | flops | bytes accessed | tf_op | source)
XLA Modules:
  0.0 1783.3 jit_solution(2049201620524090755)
XLA Ops:
  9.7 54.1 %collective-permute-done = bf16[384,6400]{1,0:T(8,128)(2,1)S(1)} collective-permute-done((bf16[384,6400]{1,0:T(8,128)(2,1)}, bf16[384,6400]{1,0:T(8,128)(2,1)S(1)}, u32[]{:S(2)}, u32[]{:S(2)}) %collective-permute-start) | collective-permute-done | bytes 4915232 | tf_op jit(solution)/shard_map/ppermute | solution.py:133
  67.8 53.7 %collective-permute-done.1 = bf16[384,6400]{1,0:T(8,128)(2,1)} collective-permute-done((bf16[384,6400]{1,0:T(8,128)(2,1)S(1)}, bf16[384,6400]{1,0:T(8,128)(2,1)}, u32[]{:S(2)}, u32[]{:S(2)}) %collective-permute-start.1) | collective-permute-done | bytes 4915232 | tf_op jit(solution)/shard_map/ppermute | solution.py:133
  124.2 55.3 %all-gather = bf16[4,1,384]{2,1,0:T(2,128)(2,1)S(1)} all-gather(bf16[1,1,384]{2,1,0:T(2,128)(2,1)S(1)} %reshape.540), channel_id=1, replica_groups=mesh['seq'=8,'fsdp'=4] {'fsdp'}, dimensions={0}, use_global_device_ids=true | all-gather | bytes 3840 | tf_op jit(solution)/shard_map/all_gather | solution.py:152
  230.1 12.8 fusion.97
  253.4 12.1 all-to-all-done.2
  308.6 74.3 %while.41 = (s32[]{:T(128)}, f32[6,64,128]{2,1,0:T(8,128)S(1)}, f32[4,256,6,64]{1,0,3,2:T(4,128)}, f32[4,6,64,128]{3,2,1,0:T(8,128)}, f32[4,256,6]{1,2,0:T(8,128...) while((s32[]{:T(128)}, f32[6,64,128]{2,1,0:T(8,128)S(1)}, ...), condition=%wide.region_4.5_spmd.clone, body=%wide.region_1.4_spmd.clone.sunk | while | flops 706957824 | bytes 5773705 | solution.py:46
  315.4 9.5 dynamic_update_slice.89
  407.9 13.6 all-to-all-done.4
  444.2 14.1 all-to-all-done.5
  473.3 169.8 %while.42 = (s32[]{:T(128)}, f32[6]{0:T(128)}, f32[6,64,128]{2,1,0:T(8,128)S(1)}, f32[4,256,6,64]{1,0,3,2:T(4,128)}, f32[4,256,6]{1,2,0:T(8,128)}, /*index=5*/f3...) while((s32[]{:T(128)}, f32[6]{0:T(128)}, ...), condition=%wide.region_20.21_spmd.clone, body=%wide.region_7.20_spmd.clone.sunk | while | flops 1669247488 | bytes 16049488 | solution.py:46
  685.9 24.3 %all_to_all.141 = bf16[8,128,384]{2,1,0:T(8,128)(2,1)S(1)} all-to-all(bf16[8,128,384]{2,1,0:T(8,128)(2,1)S(1)} %bitcast.588), channel_id=1, replica_groups=mesh['seq'=8,'fsdp'=4] {'seq'}, dimensions={0} | all-to-all | bytes 1572864 | tf_op jit(solution)/shard_map/all_to_all | solution.py:251
  716.0 19.5 %all-to-all-done.6 = bf16[8,128,384]{2,1,0:T(8,128)(2,1)S(1)} async-done(((bf16[8,128,384]{2,1,0:T(8,128)(2,1)}), bf16[8,128,384]{2,1,0:T(8,128)(2,1)S(1)}, u32[]{:S(2)}, u32[]{:S(2)}) %all-to-all-start.6) | async-done | bytes 786464 | tf_op jit(solution)/shard_map/all_to_all | solution.py:248
  737.7 14.0 fusion.126
  755.2 19.5 %convolution_bitcast_fusion.2 = f32[8,4,48,6400]{3,2,0,1:T(8,128)} fusion(bf16[4,8,48,128]{3,2,1,0:T(8,128)(2,1)} %bitcast.579, bf16[128,6400]{1,0:T(8,128)(2,1)S(1)} %constant_dynamic-update-slice_fusion.8), kind=kOutput, calls=%fused_computation.128 | convolution fusion | flops 2516582400 | bytes 41353216 | tf_op jit(solution)/shard_map/dot_general | solution.py:94
  774.7 28.4 %copy.323 = f32[8,4,48,6400]{3,2,1,0:T(8,128)} copy(f32[8,4,48,6400]{3,2,0,1:T(8,128)} %convolution_bitcast_fusion.2) | data formatting | bytes 78643200 | tf_op jit(solution)/shard_map/transpose | solution.py:102
  812.4 129.1 %reduce-scatter.12.cloned.1.call-done = f32[96,1536]{1,0:T(8,128)} async-done(((f32[3072,1536]{1,0:T(8,128)}), f32[96,1536]{1,0:T(8,128)}) %reduce-scatter.12.cloned.1.call-update) | async-done | bytes 589840 | tf_op jit(solution)/shard_map/reduce_scatter | solution.py:335
  941.5 364.1 %reduce-scatter.10.cloned.1.call-done = f32[48,6400]{1,0:T(8,128)} async-done(((f32[1536,6400]{1,0:T(8,128)}), f32[48,6400]{1,0:T(8,128)}) %reduce-scatter.10.cloned.1.call-update) | async-done | bytes 1228816 | tf_op jit(solution)/shard_map/reduce_scatter | solution.py:292
  1314.2 123.8 %all-reduce.33.cloned.1.call-done = (f32[4,3328]{1,0:T(4,128)}, f32[3328]{0:T(1024)}, f32[384]{0:T(512)}, f32[384]{0:T(512)}, f32[384]{0:T(512)}, /*index=5*/f32[3072]{0:T(1024)}, f32[1536]{0:T(1024)}) async-done(((f32[4,3328]{1,0:T(4,128)}, f32[3328]{0:T(1024)}, f32[384]{0:T(512)}, f32[384]{0:T(512)}, f32[384]{0:T(512)}, /*index=5*/f32[3072]{0:T(1024)}, f32[1536]{0:T(1024)}), (f32[4,3328]{1,0:T(4,128)}, ...) | async-done | bytes 89616
  1438.8 27.0 %all-gather.3 = f32[8,104,4]{1,2,0:T(4,128)S(1)} all-gather(f32[1,104,4]{1,2,0:T(4,128)S(1)} %dynamic-slice_bitcast_fusion.7), channel_id=1, replica_groups=mesh['seq'=8,'fsdp'=4] {'seq'}, dimensions={0}, use_global_device_ids=true | all-gather | bytes 14976 | tf_op jit(solution)/shard_map/all_gather | solution.py:345
  1472.8 35.5 %all-reduce.29 = (f32[832]{0:T(1024)}, f32[768]{0:T(1024)}, f32[384]{0:T(512)}) all-reduce(f32[832]{0:T(1024)S(1)} %dynamic-slice_dynamic-update-slice_fusion.2, f32[768]{0:T(1024)S(1)} %dynamic-slice_dynamic-update-slice_fusion.1, f32[384]{0:T(512)S(1)} %dynamic-slice_dynamic-update-slice_fusion), channel_id=1, replica_groups=mesh['seq'=8,'fsdp'=4] {'seq'}, use_global_device_ids=true, to_apply=%add.18 | all-reduce | flops 1984 | bytes 15872
  1508.3 32.6 %reduce-scatter.14.cloned.1.call-done = f32[48,48]{1,0:T(8,128)} async-done(((f32[1536,48]{1,0:T(8,128)}), f32[48,48]{1,0:T(8,128)}) %reduce-scatter.14.cloned.1.call-update) | async-done | bytes 9232 | tf_op jit(solution)/shard_map/reduce_scatter | solution.py:298
  1541.0 32.1 %all_gather.58 = f32[384,48]{1,0:T(8,128)S(1)} all-gather(f32[48,48]{1,0:T(8,128)} %reduce-scatter.14.cloned.1.call-done), channel_id=1, replica_groups=mesh['seq'=8,'fsdp'=4] {'seq'}, dimensions={0}, use_global_device_ids=true | all-gather | bytes 82944 | tf_op jit(solution)/shard_map/all_gather | solution.py:344
  1573.8 48.8 %all-gather.12.cloned.1.call-done = f32[768,1536]{1,0:T(8,128)} async-done(((f32[96,1536]{1,0:T(8,128)}), f32[768,1536]{1,0:T(8,128)}) %all-gather.12.cloned.1.call-update) | async-done | bytes 4718608 | tf_op jit(solution)/shard_map/all_gather | solution.py:349
  1622.6 142.8 %all-gather.10.cloned.1.call-done = f32[384,6400]{1,0:T(8,128)} async-done(((f32[48,6400]{1,0:T(8,128)}), f32[384,6400]{1,0:T(8,128)}) %all-gather.10.cloned.1.call-update) | async-done | bytes 9830416 | tf_op jit(solution)/shard_map/all_gather | solution.py:343
  (703 shorter events, 496.1 us)
Async XLA Ops:
  7.2 56.6 %collective-permute-start = (bf16[384,6400]{1,0:T(8,128)(2,1)}, bf16[384,6400]{1,0:T(8,128)(2,1)S(1)}, u32[]{:S(2)}, u32[]{:S(2)}) collective-permute-start(bf16[384,6400]{1,0:T(8,128)(2,1)} %param.17), channel_id=1, source_target_pairs={{0,3},{1,0},{2,1},{3,2},{4,7},{5,4},{6,5},{7,6},{8,11},{9,8},{10,9... | collective-permute-start | bytes 14745608 | tf_op jit(solution)/shard_map/ppermute | solution.py:133
  66.0 55.5 %collective-permute-start.1 = (bf16[384,6400]{1,0:T(8,128)(2,1)S(1)}, bf16[384,6400]{1,0:T(8,128)(2,1)}, u32[]{:S(2)}, u32[]{:S(2)}) collective-permute-start(bf16[384,6400]{1,0:T(8,128)(2,1)S(1)} %collective-permute-done), channel_id=1, source_target_pairs={{0,3},{1,0},{2,1},{3,2},{4,7},{5,4},{6,5},{7,6},{8,11},{9,8},{10,9... | collective-permute-start | bytes 14745608 | tf_op jit(solution)/shard_map/ppermute | solution.py:133
  121.5 87.5 %collective-permute-start.2 = (bf16[384,6400]{1,0:T(8,128)(2,1)}, bf16[384,6400]{1,0:T(8,128)(2,1)}, u32[]{:S(2)}, u32[]{:S(2)}) collective-permute-start(bf16[384,6400]{1,0:T(8,128)(2,1)} %collective-permute-done.1), channel_id=1, source_target_pairs={{0,3},{1,0},{2,1},{3,2},{4,7},{5,4},{6,5},{7,6},{8,11},{9,8},{10,9... | collective-permute-start | bytes 14745608 | tf_op jit(solution)/shard_map/ppermute | solution.py:133
  188.9 55.2 %all-to-all-start = ((bf16[128,8,6]{0,2,1:T(8,128)(2,1)}), bf16[128,8,6]{0,2,1:T(8,128)(2,1)S(1)}, u32[]{:S(2)}, u32[]{:S(2)}) async-start(bf16[128,8,6]{0,2,1:T(8,128)(2,1)} %all_to_all.106), calls=%async_computation | async-start | bytes 32768 | tf_op jit(solution)/shard_map/all_to_all | solution.py:191
  194.7 227.4 %all-gather.8.cloned.1.call-start = ((), (), s32[]{:S(2)}) async-start(), calls=%async_computation.13 | async-start | bytes 11796480 | tf_op jit(solution)/shard_map/all_gather | solution.py:153
  244.9 20.5 %all-to-all-start.2 = ((bf16[128,8,256]{2,0,1:T(8,128)(2,1)}), bf16[128,8,256]{2,0,1:T(8,128)(2,1)S(1)}, u32[]{:S(2)}, u32[]{:S(2)}) async-start(bf16[128,8,256]{2,0,1:T(8,128)(2,1)} %tile.28), calls=%async_computation.2 | async-start | bytes 1048576 | tf_op jit(solution)/shard_map/all_to_all | solution.py:192
  265.4 24.0 %all-to-all-start.1 = ((bf16[128,8,384]{2,0,1:T(8,128)(2,1)}), bf16[128,8,384]{2,0,1:T(8,128)(2,1)S(1)}, u32[]{:S(2)}, u32[]{:S(2)}) async-start(bf16[128,8,384]{2,0,1:T(8,128)(2,1)} %bitcast.416), calls=%async_computation.1 | async-start | bytes 1572864 | tf_op jit(solution)/shard_map/all_to_all | solution.py:184
  284.7 154.0 %copy-start.73 = (f32[48]{0:T(128)}, f32[48]{0:T(128)S(1)}, u32[]{:S(2)}) copy-start(f32[48]{0:T(128)S(1)} %convert_element_type.138) | copy-start | bytes 580
  289.5 98.6 %all-to-all-start.3 = ((bf16[128,8,384]{0,2,1:T(8,128)(2,1)}), bf16[128,8,384]{0,2,1:T(8,128)(2,1)}, u32[]{:S(2)}, u32[]{:S(2)}) async-start(bf16[128,8,384]{0,2,1:T(8,128)(2,1)} %bitcast.18), calls=%async_computation.3 | async-start | bytes 1572864 | tf_op jit(solution)/shard_map/all_to_all | solution.py:183
  396.3 25.2 %all-to-all-start.4 = ((bf16[8,128,384]{2,1,0:T(8,128)(2,1)}), bf16[8,128,384]{2,1,0:T(8,128)(2,1)S(1)}, u32[]{:S(2)}, u32[]{:S(2)}) async-start(bf16[8,128,384]{2,1,0:T(8,128)(2,1)} %bitcast.582), calls=%async_computation.4 | async-start | bytes 1572864 | tf_op jit(solution)/shard_map/all_to_all | solution.py:224
  434.4 23.9 %all-to-all-start.5 = ((bf16[128,8,384]{0,2,1:T(8,128)(2,1)}), bf16[128,8,384]{0,2,1:T(8,128)(2,1)}, u32[]{:S(2)}, u32[]{:S(2)}) async-start(bf16[128,8,384]{0,2,1:T(8,128)(2,1)} %bitcast.585), calls=%async_computation.5 | async-start | bytes 1572864 | tf_op jit(solution)/shard_map/all_to_all | solution.py:237
  438.6 298.2 %reduce-scatter.8.cloned.1.call-start = ((), (), s32[]{:S(2)}) async-start(), calls=%async_computation.14 | async-start | bytes 589824 | tf_op jit(solution)/shard_map/reduce_scatter | solution.py:262
  663.8 277.7 %reduce-scatter.12.cloned.1.call-start = ((), (), s32[]{:S(2)}) async-start(), calls=%async_computation.17 | async-start | bytes 19464192 | tf_op jit(solution)/shard_map/reduce_scatter | solution.py:335
  675.8 10.1 all-to-all-start.8
  710.2 25.4 %all-to-all-start.6 = ((bf16[8,128,384]{2,1,0:T(8,128)(2,1)}), bf16[8,128,384]{2,1,0:T(8,128)(2,1)S(1)}, u32[]{:S(2)}, u32[]{:S(2)}) async-start(bf16[8,128,384]{2,1,0:T(8,128)(2,1)} %bitcast.29), calls=%async_computation.6 | async-start | bytes 1572864 | tf_op jit(solution)/shard_map/all_to_all | solution.py:248
  713.8 591.9 %reduce-scatter.10.cloned.1.call-start = ((), (), s32[]{:S(2)}) async-start(), calls=%async_computation.15 | async-start | bytes 40550400 | tf_op jit(solution)/shard_map/reduce_scatter | solution.py:292
  803.2 634.9 %all-reduce.33.cloned.1.call-start = ((), (), s32[]{:S(2)}) async-start(), calls=%async_computation.20 | async-start | bytes 192512
  811.0 730.0 %reduce-scatter.14.cloned.1.call-start = ((), (), s32[]{:S(2)}) async-start(), calls=%async_computation.19 | async-start | bytes 811008 | tf_op jit(solution)/shard_map/reduce_scatter | solution.py:298
  812.3 493.4 %copy-start.81 = (u32[32]{0:T(128)S(1)}, u32[32]{0:T(128)}, u32[]{:S(2)}) copy-start(u32[32]{0:T(128)} %constant.221) | copy-start | bytes 388
  812.3 496.0 %copy-start.28 = (bf16[1,128,1536]{2,1,0:T(8,128)(2,1)S(1)}, bf16[1,128,1536]{2,1,0:T(8,128)(2,1)}, u32[]{:S(2)}) copy-start(bf16[1,128,1536]{2,1,0:T(8,128)(2,1)} %param.16) | copy-start | bytes 1179652
  812.3 496.0 %copy-start.37 = (f32[4,1,768]{2,1,0:T(1,128)S(1)}, f32[4,1,768]{2,1,0:T(1,128)}, u32[]{:S(2)}) copy-start(f32[4,1,768]{2,1,0:T(1,128)} %copy-done.36) | copy-start | bytes 36868
  812.3 496.0 %copy-start.67 = (f32[128]{0:T(128)S(1)}, f32[128]{0:T(128)}, u32[]{:S(2)}) copy-start(f32[128]{0:T(128)} %copy-done.66) | copy-start | bytes 1540
  812.3 810.3 %all-gather.12.cloned.1.call-start = ((), (), s32[]{:S(2)}) async-start(), calls=%async_computation.18 | async-start | bytes 5308416 | tf_op jit(solution)/shard_map/all_gather | solution.py:349
  941.5 823.9 %all-gather.10.cloned.1.call-start = ((), (), s32[]{:S(2)}) async-start(), calls=%async_computation.16 | async-start | bytes 11059200 | tf_op jit(solution)/shard_map/all_gather | solution.py:343
  (106 other events, 929.4 us)
Sparse Core Ops, SparseCore 0:
  197.1 65.5 all-gather.7
  663.9 62.6 reduce-scatter.7
  733.0 208.4 reduce-scatter.11
  947.8 357.8 reduce-scatter.9
  1313.1 124.8 all-reduce.32
  1443.6 97.3 reduce-scatter.13
  1543.2 79.3 all-gather.11
  1624.8 140.5 all-gather.9
